TPU v7x, 32 devices: a whole 2x2x4 slice. The times are simulated.
32 devices in a mesh: pr: 4 (over y, x), pc: 8 (over z, core).
Axes of the slice: x: 2, y: 2, z: 4, core: 2. Of those that a mesh axis runs over, the one named last changes fastest.
Arguments:
- pair_state: bfloat16 [96, 96, 128], P('pr', 'pc'), may hold values from -6 to 6
- left_weight: bfloat16 [128, 128], replicated, may hold values from -0.5 to 0.5
- right_weight: bfloat16 [128, 128], replicated, may hold values from -0.5 to 0.5
- mid_gain: float32 [128], replicated, may hold values from 0.25 to 1.75
- out_weight: bfloat16 [128, 128], replicated, may hold values from -0.5 to 0.5
- out_gate: bfloat16 [128, 128], replicated, may hold values from -0.5 to 0.5
Outputs:
- pair_update: bfloat16 [96, 96, 128], P('pr', 'pc')
All inputs are finite; a program needn't handle non-finite values.
Results may differ from a plain program's by a relative error of at most 0.012.
Values may be sent and summed in bfloat16 or wider, within the bound.
A program may use at most 128 MiB of HBM per device.

v0:
```python
import jax
import jax.numpy as jnp
from jax import lax
from jax.sharding import PartitionSpec as P


def scale_channels(values, channel_gain):
    centred = values - jnp.mean(values, axis=-1, keepdims=True)
    return (
        centred
        * lax.rsqrt(jnp.mean(centred * centred, axis=-1, keepdims=True) + 1e-05)
        * channel_gain
    )


def project_pair(pair_in, left_weight, right_weight):
    left = jnp.einsum("ijc,cd->ijd", pair_in, left_weight, preferred_element_type=jnp.float32)
    right = jnp.einsum("ijc,cd->ijd", pair_in, right_weight, preferred_element_type=jnp.float32)
    return (pair_in, left.astype(jnp.bfloat16), right.astype(jnp.bfloat16))


def close_update(mixed, ready, mid_gain, out_weight, out_gate):
    scaled = scale_channels(mixed.astype(jnp.float32), mid_gain).astype(jnp.bfloat16)
    scaled = lax.optimization_barrier(scaled)
    gate = jax.nn.sigmoid(
        jnp.einsum("ijc,cd->ijd", ready, out_gate, preferred_element_type=jnp.float32)
    )
    return (
        jnp.einsum("ijd,dc->ijc", scaled, out_weight, preferred_element_type=jnp.float32) * gate
    ).astype(jnp.bfloat16)


def body(pair_state, left_weight, right_weight, mid_gain, out_weight, out_gate):
    ready, left, right = project_pair(pair_state, left_weight, right_weight)
    count = pair_state.shape[0] * lax.axis_size("pr")
    left_lines, right_lines = (
        lax.all_to_all(left, "pr", split_axis=2, concat_axis=0, tiled=True),
        lax.all_to_all(right, "pr", split_axis=2, concat_axis=0, tiled=True),
    )
    strip = jnp.einsum(
        "kid,kjd->ijd",
        lax.all_gather(left_lines, "pc", axis=1, tiled=True),
        right_lines,
        preferred_element_type=jnp.float32,
    )
    strip = (strip * count ** (-0.5)).astype(jnp.bfloat16)
    mixed = lax.all_to_all(strip, "pr", split_axis=0, concat_axis=2, tiled=True)
    return close_update(mixed, ready, mid_gain, out_weight, out_gate)


def solution(mesh):
    placed = (P("pr", "pc", None), P(), P(), P(), P(), P())
    return jax.shard_map(
        body, mesh=mesh, in_specs=placed, out_specs=P("pr", "pc", None), check_vma=False
    )
```

profile of v0, /device:TPU:0, one launch (start us, length us, event | category | flops | bytes accessed | tf_op | source)
XLA Modules:
  0.0 52.5 jit_solution(6551884356601724737)
XLA Ops:
  0.0 0.9 %copy-done = bf16[24,12,128]{2,0,1:T(8,128)(2,1)S(1)} copy-done((bf16[24,12,128]{2,0,1:T(8,128)(2,1)S(1)}, bf16[24,12,128]{2,0,1:T(8,128)(2,1)}, u32[]{:S(2)}) %copy-start) | copy-done | bytes 73752
  0.9 0.9 %convolution_convert_fusion.1 = bf16[24,12,128]{2,0,1:T(8,128)(2,1)S(1)} fusion(bf16[24,12,128]{2,0,1:T(8,128)(2,1)S(1)} %copy-done, bf16[128,128]{1,0:T(8,128)(2,1)} %param.8), kind=kOutput, calls=%fused_computation.10 | convolution fusion | flops 9474048 | bytes 180224 | tf_op jit(solution)/shard_map/ijc,cd->ijd/dot_general | solution.py:18
  1.8 0.4 copy.39
  2.3 1.1 %reshape.28 = bf16[4,2,4608]{2,1,0:T(2,128)(2,1)} reshape(bf16[128,12,24]{2,1,0:T(8,128)(2,1)S(1)} %bitcast.44) | data formatting | bytes 147456
  3.4 5.3 %all-to-all-start = ((bf16[4,2,4608]{2,1,0:T(2,128)(2,1)}), bf16[4,2,4608]{2,1,0:T(2,128)(2,1)S(1)}, u32[]{:S(2)}, u32[]{:S(2)}) async-start(bf16[4,2,4608]{2,1,0:T(2,128)(2,1)} %reshape.28), calls=%async_computation | async-start | bytes 147456 | tf_op jit(solution)/shard_map/all_to_all | solution.py:38
  8.9 0.4 copy.41
  9.3 1.1 %reshape.26 = bf16[4,2,4608]{2,1,0:T(2,128)(2,1)} reshape(bf16[128,12,24]{2,1,0:T(8,128)(2,1)S(1)} %bitcast.45) | data formatting | bytes 147456
  10.5 3.1 %all-to-all-done = bf16[4,2,4608]{2,1,0:T(2,128)(2,1)S(1)} async-done(((bf16[4,2,4608]{2,1,0:T(2,128)(2,1)}), bf16[4,2,4608]{2,1,0:T(2,128)(2,1)S(1)}, u32[]{:S(2)}, u32[]{:S(2)}) %all-to-all-start) | async-done | bytes 73760 | tf_op jit(solution)/shard_map/all_to_all | solution.py:38
  13.6 3.3 %all-to-all-start.1 = ((bf16[4,2,4608]{2,1,0:T(2,128)(2,1)}), bf16[4,2,4608]{2,1,0:T(2,128)(2,1)S(1)}, u32[]{:S(2)}, u32[]{:S(2)}) async-start(bf16[4,2,4608]{2,1,0:T(2,128)(2,1)} %reshape.26), calls=%async_computation.1 | async-start | bytes 147456 | tf_op jit(solution)/shard_map/all_to_all | solution.py:37
  16.9 0.6 %reshape.29 = bf16[128,12,24]{2,1,0:T(8,128)(2,1)S(1)} reshape(bf16[4,2,4608]{2,1,0:T(2,128)(2,1)S(1)} %all-to-all-done) | data formatting | bytes 147456
  17.5 0.3 copy.55
  18.0 3.7 %all-to-all-done.1 = bf16[4,2,4608]{2,1,0:T(2,128)(2,1)S(1)} async-done(((bf16[4,2,4608]{2,1,0:T(2,128)(2,1)}), bf16[4,2,4608]{2,1,0:T(2,128)(2,1)S(1)}, u32[]{:S(2)}, u32[]{:S(2)}) %all-to-all-start.1) | async-done | bytes 73760 | tf_op jit(solution)/shard_map/all_to_all | solution.py:37
  21.7 0.6 %reshape.27 = bf16[128,12,24]{2,1,0:T(8,128)(2,1)S(1)} reshape(bf16[4,2,4608]{2,1,0:T(2,128)(2,1)S(1)} %all-to-all-done.1) | data formatting | bytes 147456
  22.3 0.3 copy.54
  22.9 16.5 %all_gather.3 = bf16[96,96,32]{0,2,1:T(8,128)(2,1)S(1)} all-gather(bf16[96,12,32]{0,2,1:T(8,128)(2,1)S(1)} %all_to_all.40), channel_id=1, replica_groups=mesh['pr'=4,'pc'=8] {'pc'}, dimensions={1}, use_global_device_ids=true | all-gather | bytes 663552 | tf_op jit(solution)/shard_map/all_gather | solution.py:42
  39.4 0.5 fusion.5
  39.9 0.4 copy.45
  40.3 0.3 reshape.30
  40.6 7.2 %all_to_all.45 = bf16[4,2,4608]{2,1,0:T(2,128)(2,1)S(1)} all-to-all(bf16[4,2,4608]{2,1,0:T(2,128)(2,1)S(1)} %reshape.30), channel_id=1, replica_groups=mesh['pr'=4,'pc'=8] {'pr'}, dimensions={0} | all-to-all | bytes 147456 | tf_op jit(solution)/shard_map/all_to_all | solution.py:47
  48.4 0.4 reshape.21
  49.8 0.4 copy-done.3
  50.3 0.6 %copy-done.2 = bf16[128,128]{1,0:T(8,128)(2,1)S(1)} copy-done((bf16[128,128]{1,0:T(8,128)(2,1)S(1)}, bf16[128,128]{1,0:T(8,128)(2,1)}, u32[]{:S(2)}) %copy-start.2) | copy-done | bytes 32792
  51.1 0.6 %copy-done.4 = bf16[128,128]{1,0:T(8,128)(2,1)S(1)} copy-done((bf16[128,128]{1,0:T(8,128)(2,1)S(1)}, bf16[128,128]{1,0:T(8,128)(2,1)}, u32[]{:S(2)}) %copy-start.4) | copy-done | bytes 32792
  51.7 0.8 %fusion.6 = bf16[24,12,128]{2,0,1:T(8,128)(2,1)} fusion(f32[24,12,128]{2,0,1:T(8,128)S(1)} %fusion.10, bf16[24,12,128]{2,0,1:T(8,128)(2,1)S(1)} %copy-done, bf16[128,128]{1,0:T(8,128)(2,1)S(1)} %copy-done.4), kind=kOutput, calls=%fused_computation.8 | convolution fusion | flops 9621504 | bytes 327680 | tf_op jit(solution)/shard_map/ijc,cd->ijd/dot_general | solution.py:26
  (19 shorter events, 2.4 us)
Async XLA Ops:
  0.0 0.9 %copy-start = (bf16[24,12,128]{2,0,1:T(8,128)(2,1)S(1)}, bf16[24,12,128]{2,0,1:T(8,128)(2,1)}, u32[]{:S(2)}) copy-start(bf16[24,12,128]{2,0,1:T(8,128)(2,1)} %param.6) | copy-start | bytes 221188
  3.4 5.3 %copy-start.1 = (bf16[128,128]{1,0:T(8,128)(2,1)S(1)}, bf16[128,128]{1,0:T(8,128)(2,1)}, u32[]{:S(2)}) copy-start(bf16[128,128]{1,0:T(8,128)(2,1)} %param.7) | copy-start | bytes 98308
  3.4 10.2 %all-to-all-start = ((bf16[4,2,4608]{2,1,0:T(2,128)(2,1)}), bf16[4,2,4608]{2,1,0:T(2,128)(2,1)S(1)}, u32[]{:S(2)}, u32[]{:S(2)}) async-start(bf16[4,2,4608]{2,1,0:T(2,128)(2,1)} %reshape.28), calls=%async_computation | async-start | bytes 147456 | tf_op jit(solution)/shard_map/all_to_all | solution.py:38
  13.6 8.1 %all-to-all-start.1 = ((bf16[4,2,4608]{2,1,0:T(2,128)(2,1)}), bf16[4,2,4608]{2,1,0:T(2,128)(2,1)S(1)}, u32[]{:S(2)}, u32[]{:S(2)}) async-start(bf16[4,2,4608]{2,1,0:T(2,128)(2,1)} %reshape.26), calls=%async_computation.1 | async-start | bytes 147456 | tf_op jit(solution)/shard_map/all_to_all | solution.py:37
  49.5 0.7 %copy-start.3 = (f32[128]{0:T(128)S(1)}, f32[128]{0:T(128)}, u32[]{:S(2)}) copy-start(f32[128]{0:T(128)} %param.9) | copy-start | bytes 1540
  50.2 0.8 %copy-start.2 = (bf16[128,128]{1,0:T(8,128)(2,1)S(1)}, bf16[128,128]{1,0:T(8,128)(2,1)}, u32[]{:S(2)}) copy-start(bf16[128,128]{1,0:T(8,128)(2,1)} %param.10) | copy-start | bytes 98308
  50.9 0.8 %copy-start.4 = (bf16[128,128]{1,0:T(8,128)(2,1)S(1)}, bf16[128,128]{1,0:T(8,128)(2,1)}, u32[]{:S(2)}) copy-start(bf16[128,128]{1,0:T(8,128)(2,1)} %param.11) | copy-start | bytes 98308
where the time goes:
time: 53.2 us; the launch traced here: 52.5 us
  blocking collectives  23.7 us (45%)
  local copies, waits for them, and re-layouts  10.1 us (19%)
  starting transfers between devices  8.61 us (16%)
  waiting for transfers between devices  6.78 us (13%)
  matrix products  2.61 us (5%)
  other arithmetic  0.54 us (1%)
    all_gather x1, blocking collectives, body(): lax.all_gather(left_lines, 'pc', axis=1, tiled=True)  16.5 us
    all_to_all x1, blocking collectives, body(): mixed = lax.all_to_all(strip, 'pr', split_axis=0, concat_axis=2, tiled=True)  7.24 us
    unnamed x16, local copies, waits for them, and re-layouts  6.51 us
    all_to_all x1, starting transfers between devices, body(): lax.all_to_all(right, 'pr', split_axis=2, concat_axis=0, tiled=True)  5.32 us
    all_to_all x1, waiting for transfers between devices, body(): lax.all_to_all(left, 'pr', split_axis=2, concat_axis=0, tiled=True)  3.68 us
    all_to_all x1, starting transfers between devices, body(): lax.all_to_all(left, 'pr', split_axis=2, concat_axis=0, tiled=True)  3.29 us
    all_to_all x1, waiting for transfers between devices, body(): lax.all_to_all(right, 'pr', split_axis=2, concat_axis=0, tiled=True)  3.1 us
  transfers between devices with their start and end apart: 2, of which 2 were waited for; matrix products, arithmetic and copies ran while one was open for 5% of the time, Pallas kernels for 0%

commit v1 on v0

--- a/solution.py
+++ b/solution.py
@@ -1,7 +1,14 @@
+import functools
+
 import jax
 import jax.numpy as jnp
 from jax import lax
+from jax.experimental import pallas as pl
+from jax.experimental.pallas import tpu as pltpu
 from jax.sharding import PartitionSpec as P
+
+VMEM_LIMIT = 48 * 1024 * 1024
+MESH = pl.DeviceIdType.MESH
 
 
 def scale_channels(values, channel_gain):
@@ -30,7 +37,7 @@
     ).astype(jnp.bfloat16)
 
 
-def body(pair_state, left_weight, right_weight, mid_gain, out_weight, out_gate):
+def plain_body(pair_state, left_weight, right_weight, mid_gain, out_weight, out_gate):
     ready, left, right = project_pair(pair_state, left_weight, right_weight)
     count = pair_state.shape[0] * lax.axis_size("pr")
     left_lines, right_lines = (
@@ -48,8 +55,191 @@
     return close_update(mixed, ready, mid_gain, out_weight, out_gate)
 
 
+def pick(table, index):
+    value = jnp.int32(table[0])
+    for place in range(1, len(table)):
+        value = jnp.where(index == place, jnp.int32(table[place]), value)
+    return value
+
+
+def kernel(
+    rows_of, line_of,
+    x_hbm, wl_hbm, wr_hbm, gain_hbm, wo_hbm, wg_hbm, o_ref,
+    xv, wl, wr, gain, wo, wg, flat, xf, xsib, zbuf, lbuf, rbuf, gate, pout, pin,
+    in_sem, x_send, x_recv, z_send, z_recv, p_send, p_recv,
+):
+    K, J, D = xv.shape
+    N = K * J
+    half = J * J
+    a = lax.axis_index("pr")
+    c = lax.axis_index("pc")
+    z, core = c // 2, c % 2
+    sib = c + 1 - 2 * core
+    order = [
+        pick([sorted((o for o in range(line_of) if o != m), key=lambda o: abs(o - m))[t] for m in range(line_of)], z)
+        for t in range(line_of - 1)
+    ]
+
+    barrier = pltpu.get_barrier_semaphore()
+    loads = [
+        pltpu.make_async_copy(s, d, in_sem.at[n])
+        for n, (s, d) in enumerate(
+            ((x_hbm, xv), (wr_hbm, wr), (wl_hbm, wl), (wg_hbm, wg), (gain_hbm, gain), (wo_hbm, wo))
+        )
+    ]
+    for load in loads:
+        load.start()
+    for other in order:
+        pl.semaphore_signal(barrier, inc=1, device_id=(a, other * 2 + core), device_id_type=MESH)
+    pl.semaphore_signal(barrier, inc=1, device_id=(a, sib), device_id_type=MESH)
+    for step in range(1, rows_of):
+        row = (a + step) % rows_of
+        pl.semaphore_signal(barrier, inc=1, device_id=(row, c), device_id_type=MESH)
+        pl.semaphore_signal(barrier, inc=1, device_id=(row, sib), device_id_type=MESH)
+
+    loads[0].wait()
+    for k in range(K):
+        flat[k * J : (k + 1) * J, :] = xv[k].astype(jnp.float32)
+    xf[...] = flat[...].astype(xf.dtype)
+    pl.semaphore_wait(barrier, line_of - 1 + 1 + 2 * (rows_of - 1))
+
+    to_sib = pltpu.make_async_remote_copy(
+        src_ref=xf, dst_ref=xsib, send_sem=x_send, recv_sem=x_recv,
+        device_id=(a, sib), device_id_type=MESH,
+    )
+    to_line = [
+        pltpu.make_async_remote_copy(
+            src_ref=xf, dst_ref=zbuf.at[z], send_sem=z_send.at[t], recv_sem=z_recv.at[z],
+            device_id=(a, other * 2 + core), device_id_type=MESH,
+        )
+        for t, other in enumerate(order)
+    ]
+    for copy in to_line:
+        copy.start()
+    to_sib.start()
+
+    for load in loads[1:]:
+        load.wait()
+    own = jnp.dot(xf[...], wr[...], preferred_element_type=jnp.float32)
+    rbuf[:, :J, :] = own.reshape(K, J, D)
+    lbuf[...] = jnp.dot(xf[...], wl[...], preferred_element_type=jnp.float32)
+    gate[...] = jax.nn.sigmoid(jnp.dot(xf[...], wg[...], preferred_element_type=jnp.float32))
+    to_sib.wait()
+    other_right = jnp.dot(xsib[...], wr[...], preferred_element_type=jnp.float32)
+    rbuf[:, J:, :] = other_right.reshape(K, J, D)
+
+    sends = []
+    for t in range(line_of):
+        if t == 0:
+            origin = z
+        else:
+            origin = order[t - 1]
+            pltpu.make_async_copy(xf, zbuf.at[origin], z_recv.at[origin]).wait()
+            lbuf[...] = jnp.dot(zbuf[origin], wl[...], preferred_element_type=jnp.float32)
+
+        def step(k, sums):
+            right = rbuf[k]
+            return tuple(
+                total + lbuf[pl.ds(k * J + i, 1), :] * right for i, total in enumerate(sums)
+            )
+
+        sums = lax.fori_loop(
+            0, K, step, tuple(jnp.zeros((2 * J, D), jnp.float32) for _ in range(J)), unroll=2
+        )
+        for i in range(J):
+            flat[i * J : (i + 1) * J, :] = sums[i][:J]
+            flat[half + i * J : half + (i + 1) * J, :] = sums[i][J:]
+        for h in range(2):
+            pout[t, h] = flat[h * half : (h + 1) * half, :].astype(pout.dtype)
+        away = pltpu.make_async_remote_copy(
+            src_ref=pout.at[t, 0], dst_ref=pin.at[a, core], send_sem=p_send.at[t, 0],
+            recv_sem=p_recv.at[a, core], device_id=(origin, c), device_id_type=MESH,
+        )
+        here = pltpu.make_async_copy(pout.at[t, 0], pin.at[a, core], p_recv.at[a, core])
+        side = pltpu.make_async_remote_copy(
+            src_ref=pout.at[t, 1], dst_ref=pin.at[a, core], send_sem=p_send.at[t, 1],
+            recv_sem=p_recv.at[a, core], device_id=(origin, sib), device_id_type=MESH,
+        )
+        pl.when(origin != a)(away.start)
+        pl.when(origin == a)(here.start)
+        side.start()
+        sends.append((origin, away, side))
+
+    for row in range(rows_of):
+        for s in range(2):
+            pltpu.make_async_copy(pout.at[0, 0], pin.at[row, s], p_recv.at[row, s]).wait()
+    for s in range(2):
+        total = pin[0, s].astype(jnp.float32)
+        for row in range(1, rows_of):
+            total += pin[row, s].astype(jnp.float32)
+        mixed = (total * (K * rows_of) ** (-0.5)).astype(jnp.bfloat16).astype(jnp.float32)
+        scaled = scale_channels(mixed, gain[...]).astype(jnp.bfloat16)
+        out = jnp.dot(scaled, wo[...], preferred_element_type=jnp.float32)
+        flat[s * half : (s + 1) * half, :] = out * gate[s * half : (s + 1) * half, :]
+    for i in range(K):
+        o_ref[i] = flat[i * J : (i + 1) * J, :].astype(o_ref.dtype)
+
+    for copy in to_line:
+        copy.wait_send()
+    for origin, away, side in sends:
+        pl.when(origin != a)(away.wait_send)
+        side.wait_send()
+
+
+def kernel_body(rows_of, line_of, pair_state, left_weight, right_weight, mid_gain, out_weight, out_gate):
+    K, J, D = pair_state.shape
+    N = K * J
+    half = J * J
+    f32, bf16 = jnp.float32, jnp.bfloat16
+    anywhere = pl.BlockSpec(memory_space=pl.ANY)
+    dma = pltpu.SemaphoreType.DMA
+    return pl.pallas_call(
+        functools.partial(kernel, rows_of, line_of),
+        out_shape=jax.ShapeDtypeStruct((K, J, D), bf16),
+        in_specs=[anywhere] * 6,
+        out_specs=pl.BlockSpec(memory_space=pltpu.VMEM),
+        scratch_shapes=[
+            pltpu.VMEM((K, J, D), bf16),
+            pltpu.VMEM((D, D), bf16),
+            pltpu.VMEM((D, D), bf16),
+            pltpu.VMEM((1, D), f32),
+            pltpu.VMEM((D, D), bf16),
+            pltpu.VMEM((D, D), bf16),
+            pltpu.VMEM((N, D), f32),
+            pltpu.VMEM((N, D), bf16),
+            pltpu.VMEM((N, D), bf16),
+            pltpu.VMEM((line_of, N, D), bf16),
+            pltpu.VMEM((N, D), f32),
+            pltpu.VMEM((K, 2 * J, D), f32),
+            pltpu.VMEM((N, D), f32),
+            pltpu.VMEM((line_of, 2, half, D), bf16),
+            pltpu.VMEM((rows_of, 2, half, D), bf16),
+            dma((6,)), dma, dma, dma((line_of,)), dma((line_of,)), dma((line_of, 2)), dma((rows_of, 2)),
+        ],
+        compiler_params=pltpu.CompilerParams(
+            collective_id=0, has_side_effects=True, vmem_limit_bytes=VMEM_LIMIT
+        ),
+    )(pair_state, left_weight, right_weight, mid_gain.reshape(1, -1), out_weight, out_gate)
+
+
+def body(rows_of, columns_of, *arrays):
+    K, J, D = arrays[0].shape
+    fits = (
+        columns_of == 2 * rows_of
+        and K == 2 * J
+        and arrays[1].shape == (D, D)
+        and D % 128 == 0
+        and J <= 16
+        and (J * J) % 16 == 0
+    )
+    if fits:
+        return kernel_body(rows_of, columns_of // 2, *arrays)
+    return plain_body(*arrays)
+
+
 def solution(mesh):
     placed = (P("pr", "pc", None), P(), P(), P(), P(), P())
     return jax.shard_map(
-        body, mesh=mesh, in_specs=placed, out_specs=P("pr", "pc", None), check_vma=False
-    )
+        functools.partial(body, mesh.shape["pr"], mesh.shape["pc"]),
+        mesh=mesh, in_specs=placed, out_specs=P("pr", "pc", None), check_vma=False,
+    )

time: 53.2 us -> 19.5 us (0.37)
  the two profiles are of different devices: /device:TPU:0 before, /device:TPU:5 now
where the time goes in v1:
time: 19.5 us; the launch traced here: 19.2 us
  Pallas kernels  17.5 us (90%)
  local copies, waits for them, and re-layouts  1.62 us (8%)
    pallas_call x1, Pallas kernels, kernel_body(): pl.pallas_call(functools.partial(kernel, rows_of, line_of), out_shape=jax...  17.5 us
    unnamed x11, local copies, waits for them, and re-layouts  0.97 us
    pallas_call x1, local copies, waits for them, and re-layouts, kernel_body(): pl.pallas_call(functools.partial(kernel, rows_of, line_of), out_shape=jax...  0.65 us

profile of v1, /device:TPU:5, one launch (start us, length us, event | category | flops | bytes accessed | tf_op | source)
XLA Modules:
  0.0 19.2 jit_solution(10492892134371133441)
XLA Ops:
  0.0 0.0 copy-start
  0.0 0.0 copy-start.1
  0.0 0.0 copy-start.2
  0.0 0.0 copy-start.3
  0.0 0.0 copy-start.4
  0.0 1.0 %copy.7.x_hbm = bf16[24,12,128]{2,1,0:T(8,128)(2,1)S(1)} copy(bf16[24,12,128]{2,0,1:T(8,128)(2,1)} %param.6) | data formatting | bytes 147456 | tf_op args[0]
  1.0 0.0 copy-done
  1.0 0.0 copy-done.1
  1.0 0.0 copy-done.2
  1.0 0.0 copy-done.3
  1.0 0.0 copy-done.4
  1.0 17.5 %shard_map.64 = bf16[24,12,128]{2,1,0:T(8,128)(2,1)S(1)} custom-call(bf16[24,12,128]{2,1,0:T(8,128)(2,1)S(1)} %copy.7.x_hbm, bf16[128,128]{1,0:T(8,128)(2,1)S(1)} %copy-done, bf16[128,128]{1,0:T(8,128)(2,1)S(1)} %copy-done.1, f32[1,128]{1,0:T(1,128)S(1)} %bitcast.1, bf16[128,128]{1,0:T(8,128)(2,1)S(1)} %copy-done.2, bf16[128,128]{1,0:T(8,128)(2,1)S(1)} %copy-done.3), custom_call_target="tpu_custom_call" | custom-call | tf_op jit(solution)/shard_map/pallas_call | solution.py:196
  18.5 0.7 %copy.8 = bf16[24,12,128]{2,0,1:T(8,128)(2,1)} copy(bf16[24,12,128]{2,1,0:T(8,128)(2,1)S(1)} %shard_map.64) | data formatting | bytes 147456 | tf_op jit(solution)/shard_map/pallas_call | solution.py:196
Async XLA Ops:
  0.0 1.0 %copy-start = (bf16[128,128]{1,0:T(8,128)(2,1)S(1)}, bf16[128,128]{1,0:T(8,128)(2,1)}, u32[]{:S(2)}) copy-start(bf16[128,128]{1,0:T(8,128)(2,1)} %wl_hbm.1) | copy-start | bytes 98308
  0.0 1.0 %copy-start.1 = (bf16[128,128]{1,0:T(8,128)(2,1)S(1)}, bf16[128,128]{1,0:T(8,128)(2,1)}, u32[]{:S(2)}) copy-start(bf16[128,128]{1,0:T(8,128)(2,1)} %wr_hbm.1) | copy-start | bytes 98308
  0.0 1.0 %copy-start.2 = (bf16[128,128]{1,0:T(8,128)(2,1)S(1)}, bf16[128,128]{1,0:T(8,128)(2,1)}, u32[]{:S(2)}) copy-start(bf16[128,128]{1,0:T(8,128)(2,1)} %wo_hbm.1) | copy-start | bytes 98308
  0.0 1.0 %copy-start.3 = (bf16[128,128]{1,0:T(8,128)(2,1)S(1)}, bf16[128,128]{1,0:T(8,128)(2,1)}, u32[]{:S(2)}) copy-start(bf16[128,128]{1,0:T(8,128)(2,1)} %wg_hbm.1) | copy-start | bytes 98308
  0.0 1.0 %copy-start.4 = (f32[128]{0:T(128)S(1)}, f32[128]{0:T(128)}, u32[]{:S(2)}) copy-start(f32[128]{0:T(128)} %param.9) | copy-start | bytes 1540

commit v2 on v0

--- a/solution.py
+++ b/solution.py
@@ -1,7 +1,14 @@
+import functools
+
 import jax
 import jax.numpy as jnp
 from jax import lax
+from jax.experimental import pallas as pl
+from jax.experimental.pallas import tpu as pltpu
 from jax.sharding import PartitionSpec as P
+
+PIECES = 3
+MESH = pl.DeviceIdType.MESH
 
 
 def scale_channels(values, channel_gain):
@@ -30,7 +37,7 @@
     ).astype(jnp.bfloat16)
 
 
-def body(pair_state, left_weight, right_weight, mid_gain, out_weight, out_gate):
+def plain_body(pair_state, left_weight, right_weight, mid_gain, out_weight, out_gate):
     ready, left, right = project_pair(pair_state, left_weight, right_weight)
     count = pair_state.shape[0] * lax.axis_size("pr")
     left_lines, right_lines = (
@@ -48,8 +55,234 @@
     return close_update(mixed, ready, mid_gain, out_weight, out_gate)
 
 
+def kernel(
+    rows_of, line_of, J,
+    x_hbm, wl_hbm, wr_hbm, gain_hbm, wo_hbm, wg_hbm, o_ref,
+    xv, wl, wr, gain, wo, wg, xsib, zbuf, lbuf, rflat, rbuf, flat, mixed, gate, pout, pin,
+    in_sem, x_send, x_recv, z_send, z_recv, r_send, p_send, p_recv,
+):
+    N, D = xv.shape[0] * xv.shape[1], xv.shape[2]
+    K = N // J
+    G = PIECES
+    I = J // G
+    part = I * J
+    a = lax.axis_index("pr")
+    c = lax.axis_index("pc")
+    z, core = c // 2, c % 2
+    sib = c + 1 - 2 * core
+    way = 1 - 2 * (z // 2)
+    near = z + way
+    far = (z - way + line_of) % line_of
+    third = (z + 2) % line_of
+    middle = ((z + 1) % line_of) // 2 == 1
+
+    barrier = pltpu.get_barrier_semaphore()
+    for other in (near, far):
+        pl.semaphore_signal(barrier, inc=1, device_id=(a, other * 2 + core), device_id_type=MESH)
+    pl.semaphore_signal(barrier, inc=1, device_id=(a, sib), device_id_type=MESH)
+    for step in range(1, rows_of):
+        row = (a + step) % rows_of
+        pl.semaphore_signal(barrier, inc=1, device_id=(row, c), device_id_type=MESH)
+        pl.semaphore_signal(barrier, inc=1, device_id=(row, sib), device_id_type=MESH)
+    loads = [
+        pltpu.make_async_copy(s, d, in_sem.at[n])
+        for n, (s, d) in enumerate(
+            ((x_hbm, xv), (wr_hbm, wr), (wl_hbm, wl), (wg_hbm, wg), (gain_hbm, gain), (wo_hbm, wo))
+        )
+    ]
+    for load in loads:
+        load.start()
+    for load in loads:
+        load.wait()
+
+    xs = xv[...].reshape(N, D)
+    own = jnp.dot(xs, wr[...], preferred_element_type=jnp.float32)
+    rflat[:N, :] = own
+    lbuf[...] = jnp.dot(xs, wl[...], preferred_element_type=jnp.float32)
+    gate[...] = jax.nn.sigmoid(jnp.dot(xs, wg[...], preferred_element_type=jnp.float32))
+
+    pl.semaphore_wait(barrier, 3 + 2 * (rows_of - 1))
+
+    def along(src, origin, g, target, sem):
+        return pltpu.make_async_remote_copy(
+            src_ref=src, dst_ref=zbuf.at[origin, g], send_sem=sem, recv_sem=z_recv.at[origin, g],
+            device_id=(a, target * 2 + core), device_id_type=MESH,
+        )
+
+    def arrived(origin, g):
+        pltpu.make_async_copy(xv.at[g], zbuf.at[origin, g], z_recv.at[origin, g]).wait()
+
+    sent = []
+    for t, target in enumerate((near, far)):
+        for g in range(G):
+            copy = along(xv.at[g], z, g, target, z_send.at[t, g])
+            copy.start()
+            sent.append(copy)
+    to_sib = pltpu.make_async_remote_copy(
+        src_ref=xv, dst_ref=xsib, send_sem=x_send, recv_sem=x_recv,
+        device_id=(a, sib), device_id_type=MESH,
+    )
+    to_sib.start()
+    to_sib.wait()
+    rflat[N:, :] = jnp.dot(xsib[...].reshape(N, D), wr[...], preferred_element_type=jnp.float32)
+    for k in range(K):
+        rbuf[k] = rflat[pl.ds(k, 2 * J, stride=K), :]
+
+    sums_sent = []
+
+    def contract(t, origin, g, base):
+        def step(k, sums):
+            right = rbuf[k]
+            return tuple(
+                total + lbuf[pl.ds(base + i * K + k, 1), :] * right for i, total in enumerate(sums)
+            )
+
+        sums = lax.fori_loop(
+            0, K, step, tuple(jnp.zeros((2 * J, D), jnp.float32) for _ in range(I)), unroll=4
+        )
+        for i in range(I):
+            flat[i * J : (i + 1) * J, :] = sums[i][:J]
+            flat[part + i * J : part + (i + 1) * J, :] = sums[i][J:]
+        for h in range(2):
+            pout[t, g, h] = flat[h * part : (h + 1) * part, :].astype(pout.dtype)
+        landing, sem = pin.at[g, core, a], p_recv.at[g, core, a]
+        away = pltpu.make_async_remote_copy(
+            src_ref=pout.at[t, g, 0], dst_ref=landing, send_sem=p_send.at[t, g, 0], recv_sem=sem,
+            device_id=(origin, c), device_id_type=MESH,
+        )
+        here = pltpu.make_async_copy(pout.at[t, g, 0], landing, sem)
+        side = pltpu.make_async_remote_copy(
+            src_ref=pout.at[t, g, 1], dst_ref=landing, send_sem=p_send.at[t, g, 1], recv_sem=sem,
+            device_id=(origin, sib), device_id_type=MESH,
+        )
+        pl.when(origin != a)(away.start)
+        pl.when(origin == a)(here.start)
+        side.start()
+        sums_sent.append((origin, away, side))
+
+    def project(origin, g):
+        block = zbuf[origin, g]
+        lbuf[: I * K, :] = jnp.dot(block, wl[...], preferred_element_type=jnp.float32)
+
+    for g in range(G):
+        contract(0, z, g, g * I * K)
+    relays = []
+    for g in range(G):
+        arrived(near, g)
+        first = along(zbuf.at[near, g], near, g, far, r_send.at[0, g])
+        second = along(zbuf.at[far, g], far, g, near, r_send.at[1, g])
+        relays += [first, second]
+
+        @pl.when(middle)
+        def _():
+            first.start()
+            arrived(far, g)
+            second.start()
+
+        project(near, g)
+        contract(1, near, g, 0)
+    for g in range(G):
+
+        @pl.when(jnp.logical_not(middle))
+        def _():
+            arrived(far, g)
+
+        project(far, g)
+        contract(2, far, g, 0)
+        arrived(third, g)
+        project(third, g)
+        contract(3, third, g, 0)
+
+    for g in range(G):
+        totals = []
+        for s in range(2):
+            for row in range(rows_of):
+                pltpu.make_async_copy(pout.at[0, 0, 0], pin.at[g, s, row], p_recv.at[g, s, row]).wait()
+            total = pin[g, s, 0].astype(jnp.float32)
+            for row in range(1, rows_of):
+                total += pin[g, s, row].astype(jnp.float32)
+            totals.append(total)
+        total = jnp.concatenate(totals, axis=0) * (K * rows_of) ** (-0.5)
+        total = total.astype(jnp.bfloat16).astype(jnp.float32)
+        scaled = scale_channels(total, gain[...]).astype(jnp.bfloat16)
+        out = jnp.dot(scaled, wo[...], preferred_element_type=jnp.float32)
+        for s in range(2):
+            for i in range(I):
+                first_row = s * part + i * J
+                mixed[pl.ds((s * G + g) * I + i, J, stride=K), :] = out[first_row : first_row + J]
+    o_ref[...] = (mixed[...] * gate[...]).astype(o_ref.dtype)
+
+    for copy in sent:
+        copy.wait_send()
+
+    @pl.when(middle)
+    def _():
+        for copy in relays:
+            copy.wait_send()
+
+    for origin, away, side in sums_sent:
+        pl.when(origin != a)(away.wait_send)
+        side.wait_send()
+
+
+def kernel_body(rows_of, line_of, pair_state, left_weight, right_weight, mid_gain, out_weight, out_gate):
+    K, J, D = pair_state.shape
+    N = K * J
+    G = PIECES
+    I = J // G
+    f32, bf16 = jnp.float32, jnp.bfloat16
+    anywhere = pl.BlockSpec(memory_space=pl.ANY)
+    dma = pltpu.SemaphoreType.DMA
+    pieces = jnp.transpose(pair_state, (1, 0, 2)).reshape(G, I * K, D)
+    update = pl.pallas_call(
+        functools.partial(kernel, rows_of, line_of, J),
+        out_shape=jax.ShapeDtypeStruct((N, D), bf16),
+        in_specs=[anywhere] * 6,
+        out_specs=pl.BlockSpec(memory_space=pltpu.VMEM),
+        scratch_shapes=[
+            pltpu.VMEM((G, I * K, D), bf16),
+            pltpu.VMEM((D, D), bf16),
+            pltpu.VMEM((D, D), bf16),
+            pltpu.VMEM((1, D), f32),
+            pltpu.VMEM((D, D), bf16),
+            pltpu.VMEM((D, D), bf16),
+            pltpu.VMEM((G, I * K, D), bf16),
+            pltpu.VMEM((line_of, G, I * K, D), bf16),
+            pltpu.VMEM((N, D), f32),
+            pltpu.VMEM((2 * N, D), f32),
+            pltpu.VMEM((K, 2 * J, D), f32),
+            pltpu.VMEM((2 * I * J, D), f32),
+            pltpu.VMEM((N, D), f32),
+            pltpu.VMEM((N, D), f32),
+            pltpu.VMEM((line_of, G, 2, I * J, D), bf16),
+            pltpu.VMEM((G, 2, rows_of, I * J, D), bf16),
+            dma((6,)), dma, dma, dma((2, G)), dma((line_of, G)), dma((2, G)),
+            dma((line_of, G, 2)), dma((G, 2, rows_of)),
+        ],
+        compiler_params=pltpu.CompilerParams(collective_id=0, has_side_effects=True),
+    )(pieces, left_weight, right_weight, mid_gain.reshape(1, -1), out_weight, out_gate)
+    return jnp.transpose(update.reshape(J, K, D), (1, 0, 2))
+
+
+def body(rows_of, columns_of, *arrays):
+    K, J, D = arrays[0].shape
+    fits = (
+        columns_of == 2 * rows_of
+        and columns_of == 8
+        and K == 2 * J
+        and arrays[1].shape == (D, D)
+        and D % 128 == 0
+        and J <= 16
+        and J % PIECES == 0
+    )
+    if fits:
+        return kernel_body(rows_of, columns_of // 2, *arrays)
+    return plain_body(*arrays)
+
+
 def solution(mesh):
     placed = (P("pr", "pc", None), P(), P(), P(), P(), P())
     return jax.shard_map(
-        body, mesh=mesh, in_specs=placed, out_specs=P("pr", "pc", None), check_vma=False
-    )
+        functools.partial(body, mesh.shape["pr"], mesh.shape["pc"]),
+        mesh=mesh, in_specs=placed, out_specs=P("pr", "pc", None), check_vma=False,
+    )

time: 53.2 us -> 17.8 us (0.33)
  the two profiles are of different devices: /device:TPU:0 before, /device:TPU:5 now
where the time goes in v2:
time: 17.8 us; the launch traced here: 17.6 us
  Pallas kernels  16.1 us (90%)
  local copies, waits for them, and re-layouts  1.52 us (9%)
    pallas_call x1, Pallas kernels, kernel_body(): pl.pallas_call(functools.partial(kernel, rows_of, line_of, J), out_shape=...  16.1 us
    unnamed x1, local copies, waits for them, and re-layouts  1.52 us

profile of v2, /device:TPU:5, one launch (start us, length us, event | category | flops | bytes accessed | tf_op | source)
XLA Modules:
  0.0 17.6 jit_solution(245631139570474345)
XLA Ops:
  0.0 16.1 %shard_map.64 = bf16[288,128]{1,0:T(8,128)(2,1)} custom-call(bf16[3,96,128]{2,1,0:T(8,128)(2,1)} %bitcast.8, bf16[128,128]{1,0:T(8,128)(2,1)} %wl_hbm.1, bf16[128,128]{1,0:T(8,128)(2,1)} %wr_hbm.1, f32[1,128]{1,0:T(1,128)} %bitcast.9, bf16[128,128]{1,0:T(8,128)(2,1)} %wo_hbm.1, bf16[128,128]{1,0:T(8,128)(2,1)} %wg_hbm.1), custom_call_target="tpu_custom_call" | custom-call | tf_op jit(solution)/shard_map/pallas_call | solution.py:237
  16.1 1.5 %copy.8 = bf16[24,12,128]{2,0,1:T(8,128)(2,1)} copy(bf16[24,12,128]{2,0,1:T(8,128)(2,1)} %bitcast.7) | data formatting | bytes 147456

commit v3 on v2

--- a/solution.py
+++ b/solution.py
@@ -7,7 +7,7 @@
 from jax.experimental.pallas import tpu as pltpu
 from jax.sharding import PartitionSpec as P
 
-PIECES = 3
+PIECES = 2
 MESH = pl.DeviceIdType.MESH
 
 
@@ -59,7 +59,7 @@
     rows_of, line_of, J,
     x_hbm, wl_hbm, wr_hbm, gain_hbm, wo_hbm, wg_hbm, o_ref,
     xv, wl, wr, gain, wo, wg, xsib, zbuf, lbuf, rflat, rbuf, flat, mixed, gate, pout, pin,
-    in_sem, x_send, x_recv, z_send, z_recv, r_send, p_send, p_recv,
+    in_sem, x_send, x_recv, z_send, z_recv, r_send, p_send, p_recv, ready, ends,
 ):
     N, D = xv.shape[0] * xv.shape[1], xv.shape[2]
     K = N // J
@@ -71,19 +71,25 @@
     z, core = c // 2, c % 2
     sib = c + 1 - 2 * core
     way = 1 - 2 * (z // 2)
+    inner = ((z + 1) % line_of) // 2
+    middle = inner == 1
     near = z + way
     far = (z - way + line_of) % line_of
     third = (z + 2) % line_of
-    middle = ((z + 1) % line_of) // 2 == 1
+    across = a + 1 - 2 * (a % 2)
+    along_y = (a + 2) % rows_of
 
     barrier = pltpu.get_barrier_semaphore()
-    for other in (near, far):
-        pl.semaphore_signal(barrier, inc=1, device_id=(a, other * 2 + core), device_id_type=MESH)
-    pl.semaphore_signal(barrier, inc=1, device_id=(a, sib), device_id_type=MESH)
-    for step in range(1, rows_of):
-        row = (a + step) % rows_of
-        pl.semaphore_signal(barrier, inc=1, device_id=(row, c), device_id_type=MESH)
-        pl.semaphore_signal(barrier, inc=1, device_id=(row, sib), device_id_type=MESH)
+
+    def greet(row, column):
+        pl.semaphore_signal(barrier, inc=1, device_id=(row, column), device_id_type=MESH)
+
+    greet(a, near * 2 + core)
+    pl.when(middle)(lambda: greet(a, far * 2 + core))
+    for row in (across, along_y):
+        greet(row, c)
+        greet(row, sib)
+    greet(a, sib)
     loads = [
         pltpu.make_async_copy(s, d, in_sem.at[n])
         for n, (s, d) in enumerate(
@@ -101,7 +107,7 @@
     lbuf[...] = jnp.dot(xs, wl[...], preferred_element_type=jnp.float32)
     gate[...] = jax.nn.sigmoid(jnp.dot(xs, wg[...], preferred_element_type=jnp.float32))
 
-    pl.semaphore_wait(barrier, 3 + 2 * (rows_of - 1))
+    pl.semaphore_wait(barrier, 6 + inner)
 
     def along(src, origin, g, target, sem):
         return pltpu.make_async_remote_copy(
@@ -112,17 +118,32 @@
     def arrived(origin, g):
         pltpu.make_async_copy(xv.at[g], zbuf.at[origin, g], z_recv.at[origin, g]).wait()
 
-    sent = []
-    for t, target in enumerate((near, far)):
-        for g in range(G):
-            copy = along(xv.at[g], z, g, target, z_send.at[t, g])
-            copy.start()
-            sent.append(copy)
     to_sib = pltpu.make_async_remote_copy(
         src_ref=xv, dst_ref=xsib, send_sem=x_send, recv_sem=x_recv,
         device_id=(a, sib), device_id_type=MESH,
     )
     to_sib.start()
+    outward = [along(xv.at[g], z, g, far, z_send.at[1, g]) for g in range(G)]
+    sent = [along(xv.at[g], z, g, near, z_send.at[0, g]) for g in range(G)]
+    for copy in sent:
+        copy.start()
+
+    pl.semaphore_signal(ready, inc=1, device_id=(across, c), device_id_type=MESH)
+
+    @pl.when(middle)
+    def _():
+        pl.semaphore_signal(ends, inc=1, device_id=(a, near * 2 + core), device_id_type=MESH)
+        for copy in outward:
+            copy.start()
+        pl.semaphore_wait(ends, 1)
+        pl.semaphore_signal(ends, inc=1, device_id=(a, far * 2 + core), device_id_type=MESH)
+
+    @pl.when(jnp.logical_not(middle))
+    def _():
+        pl.semaphore_wait(ends, 1)
+        for copy in outward:
+            copy.start()
+
     to_sib.wait()
     rflat[N:, :] = jnp.dot(xsib[...].reshape(N, D), wr[...], preferred_element_type=jnp.float32)
     for k in range(K):
@@ -164,6 +185,7 @@
         block = zbuf[origin, g]
         lbuf[: I * K, :] = jnp.dot(block, wl[...], preferred_element_type=jnp.float32)
 
+    pl.semaphore_wait(ready, 1)
     for g in range(G):
         contract(0, z, g, g * I * K)
     relays = []
@@ -213,6 +235,9 @@
     o_ref[...] = (mixed[...] * gate[...]).astype(o_ref.dtype)
 
     for copy in sent:
+        copy.wait_send()
+
+    for copy in outward:
         copy.wait_send()
 
     @pl.when(middle)
@@ -257,7 +282,8 @@
             pltpu.VMEM((line_of, G, 2, I * J, D), bf16),
             pltpu.VMEM((G, 2, rows_of, I * J, D), bf16),
             dma((6,)), dma, dma, dma((2, G)), dma((line_of, G)), dma((2, G)),
-            dma((line_of, G, 2)), dma((G, 2, rows_of)),
+            dma((line_of, G, 2)), dma((G, 2, rows_of)), pltpu.SemaphoreType.REGULAR,
+            pltpu.SemaphoreType.REGULAR,
         ],
         compiler_params=pltpu.CompilerParams(collective_id=0, has_side_effects=True),
     )(pieces, left_weight, right_weight, mid_gain.reshape(1, -1), out_weight, out_gate)

time: 17.8 us -> 17.4 us (0.978)
  Pallas kernels: 16.1 us -> 15.7 us
    pallas_call x1, Pallas kernels: 16.1 us -> 15.7 us  [kernel_body(): pl.pallas_call(functools.partial(kernel, rows_of, line_of, J), out_shape=...]
where the time goes in v3:
time: 17.4 us; the launch traced here: 17.3 us
  Pallas kernels  15.7 us (90%)
  local copies, waits for them, and re-layouts  1.52 us (9%)
    pallas_call x1, Pallas kernels, kernel_body(): pl.pallas_call(functools.partial(kernel, rows_of, line_of, J), out_shape=...  15.7 us
    unnamed x1, local copies, waits for them, and re-layouts  1.52 us

profile of v3, /device:TPU:5, one launch (start us, length us, event | category | flops | bytes accessed | tf_op | source)
XLA Modules:
  0.0 17.3 jit_solution(5537007656745235818)
XLA Ops:
  0.0 15.7 %shard_map.64 = bf16[288,128]{1,0:T(8,128)(2,1)} custom-call(bf16[2,144,128]{2,1,0:T(8,128)(2,1)} %bitcast.8, bf16[128,128]{1,0:T(8,128)(2,1)} %wl_hbm.1, bf16[128,128]{1,0:T(8,128)(2,1)} %wr_hbm.1, f32[1,128]{1,0:T(1,128)} %bitcast.9, bf16[128,128]{1,0:T(8,128)(2,1)} %wo_hbm.1, bf16[128,128]{1,0:T(8,128)(2,1)} %wg_hbm.1), custom_call_target="tpu_custom_call" | custom-call | tf_op jit(solution)/shard_map/pallas_call | solution.py:262
  15.7 1.5 %copy.8 = bf16[24,12,128]{2,0,1:T(8,128)(2,1)} copy(bf16[24,12,128]{2,0,1:T(8,128)(2,1)} %bitcast.7) | data formatting | bytes 147456

commit v4 on v3

--- a/solution.py
+++ b/solution.py
@@ -159,7 +159,7 @@
             )
 
         sums = lax.fori_loop(
-            0, K, step, tuple(jnp.zeros((2 * J, D), jnp.float32) for _ in range(I)), unroll=4
+            0, K, step, tuple(jnp.zeros((2 * J, D), jnp.float32) for _ in range(I)), unroll=K
         )
         for i in range(I):
             flat[i * J : (i + 1) * J, :] = sums[i][:J]
@@ -201,6 +201,7 @@
             arrived(far, g)
             second.start()
 
+    for g in range(G):
         project(near, g)
         contract(1, near, g, 0)
     for g in range(G):

time: 17.4 us -> 17.3 us (level)
  Pallas kernels: 15.7 us -> 15.5 us
    pallas_call x1, Pallas kernels: 15.7 us -> 15.5 us  [kernel_body(): pl.pallas_call(functools.partial(kernel, rows_of, line_of, J), out_shape=...]
where the time goes in v4:
time: 17.3 us; the launch traced here: 17.1 us
  Pallas kernels  15.5 us (90%)
  local copies, waits for them, and re-layouts  1.52 us (9%)
    pallas_call x1, Pallas kernels, kernel_body(): pl.pallas_call(functools.partial(kernel, rows_of, line_of, J), out_shape=...  15.5 us
    unnamed x1, local copies, waits for them, and re-layouts  1.52 us

profile of v4, /device:TPU:5, one launch (start us, length us, event | category | flops | bytes accessed | tf_op | source)
XLA Modules:
  0.0 17.1 jit_solution(11651586558168449053)
XLA Ops:
  0.0 15.5 %shard_map.64 = bf16[288,128]{1,0:T(8,128)(2,1)} custom-call(bf16[2,144,128]{2,1,0:T(8,128)(2,1)} %bitcast.8, bf16[128,128]{1,0:T(8,128)(2,1)} %wl_hbm.1, bf16[128,128]{1,0:T(8,128)(2,1)} %wr_hbm.1, f32[1,128]{1,0:T(1,128)} %bitcast.9, bf16[128,128]{1,0:T(8,128)(2,1)} %wo_hbm.1, bf16[128,128]{1,0:T(8,128)(2,1)} %wg_hbm.1), custom_call_target="tpu_custom_call" | custom-call | tf_op jit(solution)/shard_map/pallas_call | solution.py:263
  15.6 1.5 %copy.8 = bf16[24,12,128]{2,0,1:T(8,128)(2,1)} copy(bf16[24,12,128]{2,0,1:T(8,128)(2,1)} %bitcast.7) | data formatting | bytes 147456

commit v5 on v4

--- a/solution.py
+++ b/solution.py
@@ -163,9 +163,7 @@
         )
         for i in range(I):
             flat[i * J : (i + 1) * J, :] = sums[i][:J]
-            flat[part + i * J : part + (i + 1) * J, :] = sums[i][J:]
-        for h in range(2):
-            pout[t, g, h] = flat[h * part : (h + 1) * part, :].astype(pout.dtype)
+        pout[t, g, 0] = flat[:part, :].astype(pout.dtype)
         landing, sem = pin.at[g, core, a], p_recv.at[g, core, a]
         away = pltpu.make_async_remote_copy(
             src_ref=pout.at[t, g, 0], dst_ref=landing, send_sem=p_send.at[t, g, 0], recv_sem=sem,
@@ -178,6 +176,9 @@
         )
         pl.when(origin != a)(away.start)
         pl.when(origin == a)(here.start)
+        for i in range(I):
+            flat[part + i * J : part + (i + 1) * J, :] = sums[i][J:]
+        pout[t, g, 1] = flat[part:, :].astype(pout.dtype)
         side.start()
         sums_sent.append((origin, away, side))
 

time: 17.3 us -> 17.3 us (level)
  no operation moved by 1% of the time
where the time goes in v5:
time: 17.3 us; the launch traced here: 17.1 us
  Pallas kernels  15.5 us (90%)
  local copies, waits for them, and re-layouts  1.52 us (9%)
    pallas_call x1, Pallas kernels, kernel_body(): pl.pallas_call(functools.partial(kernel, rows_of, line_of, J), out_shape=...  15.5 us
    unnamed x1, local copies, waits for them, and re-layouts  1.52 us

profile of v5, /device:TPU:5, one launch (start us, length us, event | category | flops | bytes accessed | tf_op | source)
XLA Modules:
  0.0 17.1 jit_solution(1205900662322492370)
XLA Ops:
  0.0 15.5 %shard_map.64 = bf16[288,128]{1,0:T(8,128)(2,1)} custom-call(bf16[2,144,128]{2,1,0:T(8,128)(2,1)} %bitcast.8, bf16[128,128]{1,0:T(8,128)(2,1)} %wl_hbm.1, bf16[128,128]{1,0:T(8,128)(2,1)} %wr_hbm.1, f32[1,128]{1,0:T(1,128)} %bitcast.9, bf16[128,128]{1,0:T(8,128)(2,1)} %wo_hbm.1, bf16[128,128]{1,0:T(8,128)(2,1)} %wg_hbm.1), custom_call_target="tpu_custom_call" | custom-call | tf_op jit(solution)/shard_map/pallas_call | solution.py:264
  15.6 1.5 %copy.8 = bf16[24,12,128]{2,0,1:T(8,128)(2,1)} copy(bf16[24,12,128]{2,0,1:T(8,128)(2,1)} %bitcast.7) | data formatting | bytes 147456
